TPU v7x, 32 devices: a whole 2x2x4 slice. The times are simulated.
32 devices in a mesh: dom: 16 (over z, y, x), sub: 2 (over core).
Axes of the slice: x: 2, y: 2, z: 4, core: 2. Of those that a mesh axis runs over, the one named last changes fastest.
Arguments:
- right_side: float32 [8, 32, 128], P(None, ('dom', 'sub')), may hold values from -18 to 18
- matrix_blocks: float32 [32, 27, 128, 128], P(('dom', 'sub')), may hold values from -1 to 2
- block_cols: int32 [32, 27], P(('dom', 'sub')), may hold values from 0 to 31, as said below
- signs: int32 [32, 128], P(('dom', 'sub')), may hold values from 0 to 1
- sample_rows: int32 [4096], replicated, may hold values from 0 to 4095, as said below
Outputs:
- solution: float32 [8, 32, 128], P(None, ('dom', 'sub'))
- residual: float32 [8, 32, 128], P(None, ('dom', 'sub'))
- basis: float32 [5, 8, 32, 128], P(None, None, ('dom', 'sub'))
Inputs may be any that keep to these rules, and one draw needn't show every extreme that they name: `block_cols`: slot 0 of every block row names the row itself; slot 1 names the row 1 before it (the row 1 after it in the first 1 row) and slot 2 the row 1 after it (the row 1 before it in the last 1 row); every other column lies in the block rows of the row's own device or of the device just before or just after it in the order of dom and sub; a column may repeat within a row. `sample_rows`: all distinct.
All inputs are finite; a program needn't handle non-finite values.
Results may differ from a plain program's by a relative error of at most 0.0003.
Values sent between devices are 32-bit elements; how exact they have to be, the bound alone decides.
A program may use at most 64 MiB of HBM per device.

v0:
```python
import functools
import math

import jax
import jax.numpy as jnp
import numpy as np
from jax import lax
from jax.experimental import pallas as pl
from jax.experimental.pallas import tpu as pltpu
from jax.sharding import PartitionSpec as P

ITERS = 5
WINDOW = 4
MESH = pl.DeviceIdType.MESH


def dct_table(block_size):
    freq = np.arange(block_size, dtype=np.float64)[:, None]
    place = np.arange(block_size, dtype=np.float64)[None, :]
    table = np.sqrt(2.0 / block_size) * np.cos(
        math.pi * (2.0 * place + 1.0) * freq / (2.0 * block_size)
    )
    factor = np.where(freq == 0.0, math.sqrt(0.5), 1.0)
    return (table * factor).astype(np.float32)


PARTS = 3


def split(value):
    pieces = []
    for _ in range(PARTS):
        rounded = value.astype(jnp.bfloat16).astype(jnp.float32)
        pieces.append(rounded)
        value = value - rounded
    return pieces


def dot_split(left, right):
    rows = left.shape[0]
    width = right.shape[0] // PARTS
    tall = jnp.concatenate(split(left), axis=0).astype(jnp.bfloat16)
    out = lax.dot_general(
        tall, right, (((1,), (1,)), ((), ())), preferred_element_type=jnp.float32
    )
    total = None
    for i in reversed(range(PARTS)):
        for k in reversed(range(PARTS - i)):
            term = out[i * rows : (i + 1) * rows, k * width : (k + 1) * width]
            total = term if total is None else total + term
    return total


def kernel(
    ndev, nsub, order_total,
    b_hbm, m_ref, cols_ref, signs_hbm, rows_hbm, table_hbm,
    out_ref,
    b_ref, signs_ref, rows_ref, table_ref,
    slots, near, own, sides, sketch, sends, heard, gathered,
    load_sem, small_sem, xsend_sem, xrecv_sem, gsend_sem, grecv_sem,
):
    nrhs, width = b_hbm.shape
    nnz = m_ref.shape[0]
    quant = width // nrhs
    me = lax.axis_index("dom") * nsub + lax.axis_index("sub")

    def place(target):
        return (target // nsub, lax.rem(target, nsub))

    barrier = pltpu.get_barrier_semaphore()

    def greet(step, carry):
        target = lax.rem(me + step, ndev)
        pl.semaphore_signal(barrier, inc=1, device_id=place(target), device_id_type=MESH)
        return carry

    lax.fori_loop(1, ndev, greet, 0, unroll=ndev <= 64)

    smalls = [
        pltpu.make_async_copy(src, dst, small_sem.at[i])
        for i, (src, dst) in enumerate(
            [(rows_hbm, rows_ref), (signs_hbm, signs_ref), (table_hbm, table_ref), (b_hbm, b_ref)]
        )
    ]
    for copy in smalls:
        copy.start()
    pieces = 3
    bounds = [nnz * p // pieces for p in range(pieces + 1)]

    def piece(p):
        span = pl.ds(bounds[p], bounds[p + 1] - bounds[p])
        return pltpu.make_async_copy(m_ref.at[span], slots.at[span], load_sem.at[p])

    for p in range(pieces):
        piece(p).start()

    @pl.when(me == 0)
    def _():
        for step in range(ITERS):
            heard[step, 0] = jnp.zeros((nrhs, width), jnp.float32)

    @pl.when(me == ndev - 1)
    def _():
        for step in range(ITERS):
            heard[step, 1] = jnp.zeros((nrhs, width), jnp.float32)

    lane = lax.broadcasted_iota(jnp.int32, (nrhs, width), 1)
    sub_id = lax.broadcasted_iota(jnp.int32, (nrhs, width), 0)

    for copy in smalls:
        copy.wait()
    wanted = me * width + lax.broadcasted_iota(jnp.int32, (8, width), 1)
    listed = rows_hbm.shape[0]
    hit = jnp.zeros((8, width), jnp.int32)
    for top in range(0, listed, 8):
        values = rows_ref[pl.ds(top, 8), :]
        for shift in range(width):
            turned = values if shift == 0 else pltpu.roll(values, shift, 1)
            hit = jnp.where(turned == wanted, 1, hit)
    kept = jnp.max(hit, axis=0, keepdims=True).astype(jnp.float32)
    flips = (2 * signs_ref[...] - 1).astype(jnp.float32)
    eye = (
        lax.broadcasted_iota(jnp.int32, (width, width), 0)
        == lax.broadcasted_iota(jnp.int32, (width, width), 1)
    )
    kept_col = jnp.sum(jnp.where(eye, kept, 0.0), axis=1, keepdims=True)
    for i, part in enumerate(split(table_ref[...] * flips * kept_col)):
        sketch[pl.ds(i * width, width), :] = part.astype(jnp.bfloat16)

    half = width // 2
    for p in range(pieces):
        piece(p).wait()
        for part in range(2):
            span = pl.ds(part * half, half)
            if p == 0:
                sums = [jnp.zeros((half, width), jnp.float32) for _ in range(3)]
            else:
                sums = [near[d, span, :] for d in range(3)]
            for slot in range(bounds[p], bounds[p + 1]):
                block = slots[slot, span, :]
                offset = cols_ref[0, slot] - me + 1
                for d in range(3):
                    share = jnp.where(offset == d, 1.0, 0.0).astype(jnp.float32)
                    sums[d] = sums[d] + share * block
            for d in range(3):
                near[d, span, :] = sums[d]

    for d, target, first in ((1, own, 0), (0, sides, 0), (2, sides, width)):
        for i, part in enumerate(split(near[d])):
            target[pl.ds(i * width, width), pl.ds(first, width)] = part.astype(jnp.bfloat16)

    pl.semaphore_wait(barrier, ndev - 1)

    def copy_to(step, side):
        target = me + 1 if side == 0 else me - 1
        return pltpu.make_async_remote_copy(
            src_ref=sends.at[step], dst_ref=heard.at[step, side],
            send_sem=xsend_sem.at[step, side], recv_sem=xrecv_sem.at[step, side],
            device_id=place(target), device_id_type=MESH,
        )

    def start_exchange(step, value):
        sends[step] = value

        @pl.when(me < ndev - 1)
        def _():
            copy_to(step, 0).start()

        @pl.when(me > 0)
        def _():
            copy_to(step, 1).start()

    def finish_exchange(step, value):
        image = dot_split(value, own[...])

        @pl.when(me > 0)
        def _():
            copy_to(step, 0).wait_recv()

        @pl.when(me < ndev - 1)
        def _():
            copy_to(step, 1).wait_recv()

        both = jnp.concatenate([heard[step, 0], heard[step, 1]], axis=1)
        return image + dot_split(both, sides[...])

    own_group = lane // quant == sub_id

    def start_sum(step, products):
        packed = jnp.zeros((nrhs, width), jnp.float32)
        for q, product in enumerate(products):
            total = jnp.sum(product, axis=1, keepdims=True)
            packed = jnp.where(lane % quant == q, total, packed)
        row = jnp.sum(jnp.where(own_group, packed, 0.0), axis=0, keepdims=True)
        gathered[step, me] = row

        def send(k, carry):
            target = lax.rem(me + k, ndev)
            pltpu.make_async_remote_copy(
                src_ref=gathered.at[step, me], dst_ref=gathered.at[step, me],
                send_sem=gsend_sem.at[step], recv_sem=grecv_sem.at[step],
                device_id=place(target), device_id_type=MESH,
            ).start()
            return carry

        lax.fori_loop(1, ndev, send, 0, unroll=ndev <= 64)

    def all_rows(step, sem):
        span = gathered.at[step, pl.ds(0, ndev - 1)]
        return pltpu.make_async_copy(span, span, sem.at[step])

    def finish_sum(step, count):
        all_rows(step, grecv_sem).wait()
        row = jnp.sum(gathered[step], axis=0)
        spread = jnp.where(own_group, jnp.broadcast_to(row, (nrhs, width)), 0.0)
        return [
            jnp.broadcast_to(
                jnp.sum(jnp.where(lane % quant == q, spread, 0.0), axis=1, keepdims=True),
                (nrhs, width),
            )
            for q in range(count)
        ]

    b = b_ref[...]
    start_exchange(0, b)
    zb = dot_split(b, sketch[...])
    image = finish_exchange(0, b)

    vs, ws, zs, ts = [], [], [], []
    vv, vw, ww = {}, {}, {}
    gram, load = {}, {}
    low, mid, diag_inv = {}, {}, {}

    def factor(i):
        for j in range(i):
            value = gram[i, j]
            for k in range(j):
                value = value - low[i, k] * low[j, k]
            low[i, j] = value * diag_inv[j]
        value = gram[i, i]
        right = load[i]
        for k in range(i):
            value = value - low[i, k] * low[i, k]
            right = right - low[i, k] * mid[k]
        diag_inv[i] = lax.rsqrt(value)
        mid[i] = right * diag_inv[i]

    def window(j):
        return range(max(0, j + 1 - WINDOW), j + 1)

    def next_scale(j):
        length_sq = ww[j, j]
        for i in window(j):
            length_sq = length_sq - 2.0 * vw[i, j] * vw[i, j]
            for k in window(j):
                length_sq = length_sq + vw[i, j] * vv[i, k] * vw[k, j]
        return lax.rsqrt(length_sq)

    def reduced(j, scale, value, parts):
        for i in window(j):
            value = value - vw[i, j] * parts[i]
        return value * scale

    def next_tables(j, scale, vt, wt, tt):
        n = j + 1
        for i in range(n):
            vv[i, n] = vv[n, i] = reduced(j, scale, vw[i, j], [vv[i, k] for k in range(n)])
            vw[i, n] = reduced(j, scale, vt[i], [vw[i, k] for k in range(n)])
            vw[n, i] = reduced(j, scale, ww[j, i], [vw[k, i] for k in range(n)])
            ww[i, n] = reduced(j, scale, wt[i], [ww[i, k] for k in range(n)])
            ww[n, i] = ww[i, n]
        vv[n, n] = one
        vw[n, n] = reduced(j, scale, ww[j, n], [vw[k, n] for k in range(n)])
        square = tt
        for i in window(j):
            square = square - 2.0 * vw[i, j] * wt[i]
            for k in window(j):
                square = square + vw[i, j] * ww[i, k] * vw[k, j]
        ww[n, n] = square * scale * scale

    one = jnp.ones((nrhs, width), jnp.float32)

    x1 = image
    start_exchange(1, x1)
    start_sum(0, [b * b, b * x1, x1 * x1])
    raw_z1 = dot_split(x1, sketch[...])
    x2 = finish_exchange(1, x1)

    start_exchange(2, x2)
    start_sum(1, [b * x2, x1 * x2, x2 * x2, raw_z1 * raw_z1, raw_z1 * zb])
    bb, by, yy = finish_sum(0, 3)
    inv_sq = 1.0 / bb
    inv = lax.rsqrt(bb)
    vs.append(b * inv)
    ws.append(x1 * inv)
    zs.append(raw_z1 * inv)
    ts.append(x2 * inv)
    vv[0, 0], vw[0, 0], ww[0, 0] = one, by * inv_sq, yy * inv_sq
    scale = next_scale(0)
    vs.append(reduced(0, scale, ws[0], vs))
    ws.append(reduced(0, scale, ts[0], ws))
    zs.append(dot_split(ws[1], sketch[...]))
    x3 = finish_exchange(2, x2)
    ts.append(reduced(0, scale, x3 * inv, ts))

    def finish_scaled(j, unit_sq, unit):
        sums = finish_sum(j, 3 * j + 2)
        sums = [value * unit_sq for value in sums[:-1]] + [sums[-1] * unit] if j == 1 else sums
        for i in range(j):
            gram[j - 1, i] = sums[2 * j + 1 + i]
        load[j - 1] = sums[3 * j + 1]
        return sums[:j], sums[j : 2 * j], sums[2 * j]

    for j in range(2, ITERS - 1):
        t = ts[j - 1]
        start_exchange(j + 1, t)
        products = [v * t for v in vs] + [w * t for w in ws] + [t * t]
        start_sum(j, products + [zs[j - 1] * z for z in zs] + [zs[j - 1] * zb])
        next_tables(j - 2, scale, *finish_scaled(j - 1, inv_sq, inv))
        scale = next_scale(j - 1)
        vs.append(reduced(j - 1, scale, ws[j - 1], vs))
        ws.append(reduced(j - 1, scale, t, ws))
        zs.append(dot_split(ws[j], sketch[...]))
        image = finish_exchange(j + 1, t)
        ts.append(reduced(j - 1, scale, image, ts))

    j = ITERS - 1
    t = ts[j - 1]
    fresh = dot_split(t, sketch[...])
    products = [zs[j - 1] * z for z in zs] + [zs[j - 1] * zb]
    products += [fresh * z for z in zs] + [fresh * zb, fresh * fresh]
    start_sum(j, products)
    next_tables(j - 2, scale, *finish_scaled(j - 1, inv_sq, inv))
    scale = next_scale(j - 1)
    vs.append(reduced(j - 1, scale, ws[j - 1], vs))
    ws.append(reduced(j - 1, scale, t, ws))
    for i in range(j - 1):
        factor(i)
    for i in range(ITERS):
        out_ref[2 + i] = vs[i] * math.sqrt(order_total)
    sums = finish_sum(j, len(products))
    for i in range(j):
        gram[j - 1, i] = gram[i, j - 1] = sums[i]
    for i in range(j - 1):
        for k in range(i):
            gram[k, i] = gram[i, k]
    load[j - 1] = sums[j]
    mixed = sums[j + 1 : 2 * j + 1]
    for i in range(j):
        gram[j, i] = reduced(j - 1, scale, mixed[i], [gram[i, k] for k in range(j)])
    load[j] = reduced(j - 1, scale, sums[2 * j + 1], load)
    square = sums[2 * j + 2]
    for i in window(j - 1):
        square = square - 2.0 * vw[i, j - 1] * mixed[i]
        for k in window(j - 1):
            square = square + vw[i, j - 1] * gram[i, k] * vw[k, j - 1]
    gram[j, j] = square * scale * scale
    factor(j - 1)
    factor(j)

    coef = {}
    for i in reversed(range(ITERS)):
        value = mid[i]
        for k in range(i + 1, ITERS):
            value = value - low[k, i] * coef[k]
        coef[i] = value * diag_inv[i]
    answer = coef[0] * vs[0]
    left_over = b - coef[0] * ws[0]
    for i in range(1, ITERS):
        answer = answer + coef[i] * vs[i]
        left_over = left_over - coef[i] * ws[i]
    out_ref[0] = answer
    out_ref[1] = left_over

    for step in range(ITERS):
        all_rows(step, gsend_sem).wait()

        @pl.when(me < ndev - 1)
        def _():
            copy_to(step, 0).wait_send()

        @pl.when(me > 0)
        def _():
            copy_to(step, 1).wait_send()


def deliver(packed_ref, sol_ref, res_ref, basis_ref):
    sol_ref[...] = packed_ref[0]
    res_ref[...] = packed_ref[1]
    basis_ref[...] = packed_ref[2:]


def per_device(ndev, nsub, right_side, matrix_blocks, block_cols, signs, sample_rows):
    nrhs, rows_dev, width = right_side.shape
    nnz = matrix_blocks.shape[1]
    order_total = ndev * rows_dev * width
    vmem = pl.BlockSpec(memory_space=pltpu.VMEM)
    anywhere = pl.BlockSpec(memory_space=pl.ANY)
    listed = sample_rows.shape[0] // width
    packed = pl.pallas_call(
        functools.partial(kernel, ndev, nsub, order_total),
        out_shape=pltpu.VMEM((ITERS + 2, nrhs, width), jnp.float32),
        in_specs=[
            anywhere, anywhere,
            pl.BlockSpec(memory_space=pltpu.SMEM),
            anywhere, anywhere, anywhere,
        ],
        out_specs=vmem,
        scratch_shapes=[
            pltpu.VMEM((nrhs, width), jnp.float32),
            pltpu.VMEM((1, width), jnp.int32),
            pltpu.VMEM((listed, width), jnp.int32),
            pltpu.VMEM((width, width), jnp.float32),
            pltpu.VMEM((nnz, width, width), jnp.float32),
            pltpu.VMEM((3, width, width), jnp.float32),
            pltpu.VMEM((PARTS * width, width), jnp.bfloat16),
            pltpu.VMEM((PARTS * width, 2 * width), jnp.bfloat16),
            pltpu.VMEM((PARTS * width, width), jnp.bfloat16),
            pltpu.VMEM((ITERS, nrhs, width), jnp.float32),
            pltpu.VMEM((ITERS, 2, nrhs, width), jnp.float32),
            pltpu.VMEM((ITERS, ndev, 1, width), jnp.float32),
            pltpu.SemaphoreType.DMA((3,)),
            pltpu.SemaphoreType.DMA((4,)),
            pltpu.SemaphoreType.DMA((ITERS, 2)),
            pltpu.SemaphoreType.DMA((ITERS, 2)),
            pltpu.SemaphoreType.DMA((ITERS,)),
            pltpu.SemaphoreType.DMA((ITERS,)),
        ],
        compiler_params=pltpu.CompilerParams(collective_id=0, has_side_effects=True),
    )(
        right_side.reshape(nrhs, width),
        matrix_blocks.reshape(nnz, width, width),
        block_cols,
        signs,
        sample_rows.reshape(-1, width),
        jnp.asarray(dct_table(width)),
    )
    answer, left_over, basis = pl.pallas_call(
        deliver,
        out_shape=(
            jax.ShapeDtypeStruct((nrhs, width), jnp.float32),
            jax.ShapeDtypeStruct((nrhs, width), jnp.float32),
            jax.ShapeDtypeStruct((ITERS, nrhs, width), jnp.float32),
        ),
        in_specs=[vmem],
        out_specs=(vmem, vmem, vmem),
    )(packed)
    return (
        answer.reshape(nrhs, rows_dev, width),
        left_over.reshape(nrhs, rows_dev, width),
        basis.reshape(ITERS, nrhs, rows_dev, width),
    )


def solution(mesh):
    nsub = mesh.shape["sub"]
    ndev = mesh.shape["dom"] * nsub
    return jax.shard_map(
        functools.partial(per_device, ndev, nsub),
        mesh=mesh,
        in_specs=(
            P(None, ("dom", "sub"), None),
            P(("dom", "sub"), None, None, None),
            P(("dom", "sub"), None),
            P(("dom", "sub"), None),
            P(),
        ),
        out_specs=(
            P(None, ("dom", "sub"), None),
            P(None, ("dom", "sub"), None),
            P(None, None, ("dom", "sub"), None),
        ),
        check_vma=False,
    )
```

profile of v0, /device:TPU:0, one launch (start us, length us, event | category | flops | bytes accessed | tf_op | source)
XLA Modules:
  0.0 30.2 jit_solution(790709058968919514)
XLA Ops:
  0.6 27.6 %shard_map.85.packed_ref = f32[7,8,128]{2,1,0:T(8,128)S(1)} custom-call(f32[8,128]{1,0:T(8,128)} %bitcast.14, f32[27,128,128]{2,1,0:T(8,128)} %bitcast.12, s32[1,27]{1,0:T(1,128)} %cols_ref.1, s32[1,128]{1,0:T(1,128)} %signs_hbm.1, s32[32,128]{1,0:T(8,128)} %bitcast.13, f32[128,128]{1,0:T(8,128)} %constant.2.clone.table_hbm), custom_call_target="tpu_custom_call" | custom-call | tf_op jit(solution)/shard_map/pallas_call | solution.py:400
  28.3 0.0 copy-start
  28.3 0.6 %copy-done = f32[7,8,128]{2,1,0:T(8,128)} copy-done((f32[7,8,128]{2,1,0:T(8,128)}, f32[7,8,128]{2,1,0:T(8,128)S(1)}, u32[]{:S(2)}) %copy-start) | copy-done | bytes 28696
  28.9 1.4 %shard_map.86 = (f32[8,128]{1,0:T(8,128)}, f32[8,128]{1,0:T(8,128)}, f32[5,8,128]{2,1,0:T(8,128)}) custom-call(f32[7,8,128]{2,1,0:T(8,128)} %copy-done), custom_call_target="tpu_custom_call" | custom-call | tf_op jit(solution)/shard_map/pallas_call | solution.py:438
Async XLA Ops:
  28.3 0.6 %copy-start = (f32[7,8,128]{2,1,0:T(8,128)}, f32[7,8,128]{2,1,0:T(8,128)S(1)}, u32[]{:S(2)}) copy-start(f32[7,8,128]{2,1,0:T(8,128)S(1)} %shard_map.85.packed_ref) | copy-start | bytes 86020
where the time goes:
time: 30.5 us; the launch traced here: 30.2 us
  Pallas kernels  29 us (95%)
  between operations  0.65 us (2%)
  local copies, waits for them, and re-layouts  0.59 us (2%)
    pallas_call x1, Pallas kernels, per_device(): pl.pallas_call(functools.partial(kernel, ndev, nsub, order_total), out_sh...  27.6 us
    pallas_call x1, Pallas kernels, per_device(): pl.pallas_call(deliver, out_shape=(jax.ShapeDtypeStruct((nrhs, width), jn...  1.36 us

commit v1 on v0

--- a/solution.py
+++ b/solution.py
@@ -384,10 +384,16 @@
             copy_to(step, 1).wait_send()
 
 
-def deliver(packed_ref, sol_ref, res_ref, basis_ref):
-    sol_ref[...] = packed_ref[0]
-    res_ref[...] = packed_ref[1]
-    basis_ref[...] = packed_ref[2:]
+def deliver(packed_ref, sol_hbm, res_hbm, basis_hbm, sem):
+    copies = [
+        pltpu.make_async_copy(packed_ref.at[0], sol_hbm, sem.at[0]),
+        pltpu.make_async_copy(packed_ref.at[1], res_hbm, sem.at[1]),
+        pltpu.make_async_copy(packed_ref.at[pl.ds(2, ITERS)], basis_hbm, sem.at[2]),
+    ]
+    for copy in copies:
+        copy.start()
+    for copy in copies:
+        copy.wait()
 
 
 def per_device(ndev, nsub, right_side, matrix_blocks, block_cols, signs, sample_rows):
@@ -443,8 +449,9 @@
             jax.ShapeDtypeStruct((ITERS, nrhs, width), jnp.float32),
         ),
         in_specs=[vmem],
-        out_specs=(vmem, vmem, vmem),
-    )(packed)
+        out_specs=(anywhere, anywhere, anywhere),
+        scratch_shapes=[pltpu.SemaphoreType.DMA((3,))],
+    )(pltpu.with_memory_space_constraint(packed, pltpu.VMEM))
     return (
         answer.reshape(nrhs, rows_dev, width),
         left_over.reshape(nrhs, rows_dev, width),

time: 30.5 us -> 29.2 us (0.957)
  Pallas kernels: 29 us -> 28.3 us
  local copies, waits for them, and re-layouts: 0.59 us -> 0 us
    pallas_call x1, Pallas kernels: 1.36 us -> 0.64 us  [per_device(): pl.pallas_call(deliver, out_shape=(jax.ShapeDtypeStruct((nrhs, width), jn...]
    unnamed x2 -> x0, local copies, waits for them, and re-layouts: 0.59 us -> none
where the time goes in v1:
time: 29.2 us; the launch traced here: 28.9 us
  Pallas kernels  28.3 us (97%)
  between operations  0.64 us (2%)
    pallas_call x1, Pallas kernels, per_device(): pl.pallas_call(functools.partial(kernel, ndev, nsub, order_total), out_sh...  27.6 us
    pallas_call x1, Pallas kernels, per_device(): pl.pallas_call(deliver, out_shape=(jax.ShapeDtypeStruct((nrhs, width), jn...  0.64 us

profile of v1, /device:TPU:0, one launch (start us, length us, event | category | flops | bytes accessed | tf_op | source)
XLA Modules:
  0.0 28.9 jit_solution(9310462562626462787)
XLA Ops:
  0.6 27.6 %shard_map.85.packed_ref = f32[7,8,128]{2,1,0:T(8,128)S(1)} custom-call(f32[8,128]{1,0:T(8,128)} %bitcast.14, f32[27,128,128]{2,1,0:T(8,128)} %bitcast.12, s32[1,27]{1,0:T(1,128)} %cols_ref.1, s32[1,128]{1,0:T(1,128)} %signs_hbm.1, s32[32,128]{1,0:T(8,128)} %bitcast.13, f32[128,128]{1,0:T(8,128)} %constant.2.clone.table_hbm), custom_call_target="tpu_custom_call" | custom-call | tf_op jit(solution)/shard_map/pallas_call | solution.py:406
  28.3 0.6 %shard_map.86 = (f32[8,128]{1,0:T(8,128)}, f32[8,128]{1,0:T(8,128)}, f32[5,8,128]{2,1,0:T(8,128)}) custom-call(f32[7,8,128]{2,1,0:T(8,128)S(1)} %shard_map.85.packed_ref), custom_call_target="tpu_custom_call" | custom-call | tf_op jit(solution)/shard_map/pallas_call | solution.py:444
